TPU v7x, 256 devices: a whole 4x4x8 slice. The times are simulated.
256 devices in a mesh: tm: 4 (over y_hi, core), anta: 32 (over x, z), antb: 2 (over y_lo).
Axes of the slice: x: 4, y: 4 (y_hi: 2, y_lo: 2; y = y_hi * 2 + y_lo), z: 8, core: 2. Of those that a mesh axis runs over, the one named last changes fastest.
Arguments:
- samples: bfloat16 [2, 512, 6144], P('antb', 'anta', 'tm'), may hold values from -6 to 6
Outputs:
- correlation: float32 [256, 2, 512, 2, 512], P('tm', None, 'anta', 'antb')
All inputs are finite; a program needn't handle non-finite values.
Results may differ from a plain program's by a relative error of at most 0.0003.
Values may be sent and summed in bfloat16 or wider, within the bound.
A program may use at most 64 MiB of HBM per device.

v0:
```python
import math

import jax
import jax.numpy as jnp
from jax import lax
from jax.sharding import PartitionSpec as P

ANTENNA_COUNT = 512
POLARISATION_NUM = 2
LAG_TOTAL = 256


def from_everyone(value, axis):
    copies = jnp.broadcast_to(value, (lax.axis_size(axis), *value.shape))
    return lax.all_to_all(copies, axis, split_axis=0, concat_axis=0, tiled=True)


def joined_along(parts, dim):
    shape = list(parts.shape[1:])
    shape[dim] *= parts.shape[0]
    return jnp.moveaxis(parts, 0, dim).reshape(shape)


def collect(value, axis, dim):
    parts = from_everyone(value, axis)
    return joined_along(parts, dim)


def lag_terms(row_padded, columns, lag_start, lag_count, window_len):
    group_len = math.gcd(lag_count, 8)
    flat_cols = columns.reshape(columns.shape[1], columns.shape[2])

    def one_group(group_index):
        first_lag = lag_start + group_index * group_len
        pieces = [
            lax.dynamic_slice_in_dim(row_padded, LAG_TOTAL - first_lag - step_index, window_len, 1)
            for step_index in range(group_len)
        ]
        stacked = jnp.stack(pieces, 0)
        return jnp.einsum("kit,jt->kij", stacked, flat_cols, preferred_element_type=jnp.float32)

    grouped = lax.map(one_group, jnp.arange(lag_count // group_len, dtype=jnp.int32))
    return grouped.reshape(lag_count, row_padded.shape[0], flat_cols.shape[0])


def collect_rows(own_window):
    return collect(own_window, "antb", 0)


def per_device(samples):
    antenna_total = samples.shape[1]
    block_len = samples.shape[2]
    tm_size = lax.axis_size("tm")
    lag_portion = LAG_TOTAL // tm_size
    full_length = block_len * tm_size
    factor = 1.0 / math.sqrt(full_length)
    lag_start = lax.axis_index("tm") * lag_portion
    whole_time = None
    whole_time = lax.all_gather(samples, "tm", axis=2, tiled=True)
    row_samples = collect_rows(whole_time)
    row_padded = jnp.pad(
        row_samples.reshape(POLARISATION_NUM * antenna_total, full_length), ((0, 0), (LAG_TOTAL, 0))
    )
    lag_group_block = lag_terms(
        row_padded,
        lax.all_gather(whole_time, "anta", axis=1, tiled=True),
        lag_start,
        lag_portion,
        full_length,
    )
    accumulated_sum = lag_group_block.reshape(
        lag_portion, POLARISATION_NUM, antenna_total, 1, ANTENNA_COUNT
    )
    return accumulated_sum * factor


def solution(mesh):
    return jax.shard_map(
        per_device,
        mesh=mesh,
        in_specs=(P("antb", "anta", "tm"),),
        out_specs=P("tm", None, "anta", "antb", None),
        check_vma=False,
    )
```

profile of v0, /device:TPU:1, one launch (start us, length us, event | category | flops | bytes accessed | tf_op | source)
XLA Modules:
  0.0 196.3 jit_solution(11786956388435641205)
XLA Ops:
  6.5 10.8 %all_gather.8 = bf16[1,16,6144]{2,1,0:T(8,128)(2,1)} all-gather(bf16[1,16,1536]{2,1,0:T(8,128)(2,1)} %param.3), channel_id=1, replica_groups=mesh['tm'=4,'anta'=32,'antb'=2] {'tm'}, dimensions={2}, use_global_device_ids=true | all-gather | bytes 245760 | tf_op jit(solution)/shard_map/all_gather | solution.py:59
  17.3 1.7 broadcast_in_dim.17
  19.0 3.5 %all-to-all-start = ((bf16[2,1,16,6144]{3,2,1,0:T(8,128)(2,1)}), bf16[2,1,16,6144]{3,2,1,0:T(8,128)(2,1)S(1)}, u32[]{:S(2)}, u32[]{:S(2)}) async-start(bf16[2,1,16,6144]{3,2,1,0:T(8,128)(2,1)} %broadcast_in_dim.17), calls=%async_computation | async-start | bytes 786432 | tf_op jit(solution)/shard_map/all_to_all | solution.py:15
  22.5 6.5 %all-to-all-done = bf16[2,1,16,6144]{3,2,1,0:T(8,128)(2,1)S(1)} async-done(((bf16[2,1,16,6144]{3,2,1,0:T(8,128)(2,1)}), bf16[2,1,16,6144]{3,2,1,0:T(8,128)(2,1)S(1)}, u32[]{:S(2)}, u32[]{:S(2)}) %all-to-all-start) | async-done | bytes 393248 | tf_op jit(solution)/shard_map/all_to_all | solution.py:15
  29.0 76.5 %all-gather.2.cloned.1.call-done = bf16[1,512,6144]{2,1,0:T(8,128)(2,1)} async-done(((bf16[1,16,6144]{2,1,0:T(8,128)(2,1)}), bf16[1,512,6144]{2,1,0:T(8,128)(2,1)}) %all-gather.2.cloned.1.call-update) | async-done | bytes 6291472 | tf_op jit(solution)/shard_map/all_gather | solution.py:66
  105.5 0.6 iota.3
  106.1 70.7 %while.14 = (s32[]{:T(128)}, f32[8,8,32,512]{3,2,1,0:T(8,128)}, s32[8]{0:T(128)}, s32[]{:T(128)}, bf16[32,6400]{1,0:T(8,128)(2,1)S(1)}, /*index=5*/bf16[512,6144...) while((s32[]{:T(128)}, f32[8,8,32,512]{3,2,1,0:T(8,128)}, ...), condition=%wide.region_1.2_spmd, body=%wide.region_0.1_spmd.sunk | while | flops 1610612736 | bytes 16254097 | solution.py:42
  106.1 1.3 dynamic_slice.107
  108.4 0.2 bitcast_dynamic-update-slice_fusion.18
  109.0 0.2 bitcast_dynamic-update-slice_fusion.21
  109.3 0.2 bitcast_dynamic-update-slice_fusion.23
  109.5 5.4 %fusion.14 = f32[8,8,32,512]{3,2,1,0:T(8,128)} fusion(f32[8,8,32,512]{3,2,1,0:T(8,128)} %get-tuple-element.216, s32[]{:T(128)} %get-tuple-element.215, bf16[8,32,6144]{2,1,0:T(8,128)(2,1)S(1)} %bitcast_dynamic-update-slice_fusion.23, bf16[512,6144]{1,0:T(8,128)(2,1)} %get-tuple-element.245), kind=kOutput, calls=%fused_computation.3.clone.1 | convolution fusion | flops 1610612736 | bytes 9961984 | tf_op jit(solution)/shard_map/while/body/eval_jaxpr/kit,jt->kij/dot_general | solution.py:40
  114.9 1.3 dynamic_slice.107
  117.0 0.2 bitcast_dynamic-update-slice_fusion.17
  117.2 0.2 bitcast_dynamic-update-slice_fusion.18
  117.6 0.2 bitcast_dynamic-update-slice_fusion.20
  117.8 0.2 bitcast_dynamic-update-slice_fusion.21
  118.2 0.2 bitcast_dynamic-update-slice_fusion.23
  118.4 5.4 %fusion.14 = f32[8,8,32,512]{3,2,1,0:T(8,128)} fusion(f32[8,8,32,512]{3,2,1,0:T(8,128)} %get-tuple-element.216, s32[]{:T(128)} %get-tuple-element.215, bf16[8,32,6144]{2,1,0:T(8,128)(2,1)S(1)} %bitcast_dynamic-update-slice_fusion.23, bf16[512,6144]{1,0:T(8,128)(2,1)} %get-tuple-element.245), kind=kOutput, calls=%fused_computation.3.clone.1 | convolution fusion | flops 1610612736 | bytes 9961984 | tf_op jit(solution)/shard_map/while/body/eval_jaxpr/kit,jt->kij/dot_general | solution.py:40
  123.8 1.3 dynamic_slice.107
  126.1 0.2 bitcast_dynamic-update-slice_fusion.18
  126.6 0.2 bitcast_dynamic-update-slice_fusion.21
  127.0 0.2 bitcast_dynamic-update-slice_fusion.23
  127.2 5.4 %fusion.14 = f32[8,8,32,512]{3,2,1,0:T(8,128)} fusion(f32[8,8,32,512]{3,2,1,0:T(8,128)} %get-tuple-element.216, s32[]{:T(128)} %get-tuple-element.215, bf16[8,32,6144]{2,1,0:T(8,128)(2,1)S(1)} %bitcast_dynamic-update-slice_fusion.23, bf16[512,6144]{1,0:T(8,128)(2,1)} %get-tuple-element.245), kind=kOutput, calls=%fused_computation.3.clone.1 | convolution fusion | flops 1610612736 | bytes 9961984 | tf_op jit(solution)/shard_map/while/body/eval_jaxpr/kit,jt->kij/dot_general | solution.py:40
  132.6 1.3 dynamic_slice.107
  135.1 0.2 bitcast_dynamic-update-slice_fusion.19
  135.7 0.2 bitcast_dynamic-update-slice_fusion.22
  136.0 5.4 %fusion.14 = f32[8,8,32,512]{3,2,1,0:T(8,128)} fusion(f32[8,8,32,512]{3,2,1,0:T(8,128)} %get-tuple-element.216, s32[]{:T(128)} %get-tuple-element.215, bf16[8,32,6144]{2,1,0:T(8,128)(2,1)S(1)} %bitcast_dynamic-update-slice_fusion.23, bf16[512,6144]{1,0:T(8,128)(2,1)} %get-tuple-element.245), kind=kOutput, calls=%fused_computation.3.clone.1 | convolution fusion | flops 1610612736 | bytes 9961984 | tf_op jit(solution)/shard_map/while/body/eval_jaxpr/kit,jt->kij/dot_general | solution.py:40
  141.4 1.3 dynamic_slice.107
  143.9 0.2 bitcast_dynamic-update-slice_fusion.19
  144.1 0.2 bitcast_dynamic-update-slice_fusion.20
  144.5 0.2 bitcast_dynamic-update-slice_fusion.22
  144.9 5.4 %fusion.14 = f32[8,8,32,512]{3,2,1,0:T(8,128)} fusion(f32[8,8,32,512]{3,2,1,0:T(8,128)} %get-tuple-element.216, s32[]{:T(128)} %get-tuple-element.215, bf16[8,32,6144]{2,1,0:T(8,128)(2,1)S(1)} %bitcast_dynamic-update-slice_fusion.23, bf16[512,6144]{1,0:T(8,128)(2,1)} %get-tuple-element.245), kind=kOutput, calls=%fused_computation.3.clone.1 | convolution fusion | flops 1610612736 | bytes 9961984 | tf_op jit(solution)/shard_map/while/body/eval_jaxpr/kit,jt->kij/dot_general | solution.py:40
  150.3 1.3 dynamic_slice.107
  152.4 0.2 bitcast_dynamic-update-slice_fusion.17
  152.9 0.2 bitcast_dynamic-update-slice_fusion.20
  153.7 5.4 %fusion.14 = f32[8,8,32,512]{3,2,1,0:T(8,128)} fusion(f32[8,8,32,512]{3,2,1,0:T(8,128)} %get-tuple-element.216, s32[]{:T(128)} %get-tuple-element.215, bf16[8,32,6144]{2,1,0:T(8,128)(2,1)S(1)} %bitcast_dynamic-update-slice_fusion.23, bf16[512,6144]{1,0:T(8,128)(2,1)} %get-tuple-element.245), kind=kOutput, calls=%fused_computation.3.clone.1 | convolution fusion | flops 1610612736 | bytes 9961984 | tf_op jit(solution)/shard_map/while/body/eval_jaxpr/kit,jt->kij/dot_general | solution.py:40
  159.1 1.3 dynamic_slice.107
  161.2 0.2 bitcast_dynamic-update-slice_fusion.17
  161.4 0.2 bitcast_dynamic-update-slice_fusion.18
  162.0 0.2 bitcast_dynamic-update-slice_fusion.21
  162.3 0.2 bitcast_dynamic-update-slice_fusion.23
  162.5 5.4 %fusion.14 = f32[8,8,32,512]{3,2,1,0:T(8,128)} fusion(f32[8,8,32,512]{3,2,1,0:T(8,128)} %get-tuple-element.216, s32[]{:T(128)} %get-tuple-element.215, bf16[8,32,6144]{2,1,0:T(8,128)(2,1)S(1)} %bitcast_dynamic-update-slice_fusion.23, bf16[512,6144]{1,0:T(8,128)(2,1)} %get-tuple-element.245), kind=kOutput, calls=%fused_computation.3.clone.1 | convolution fusion | flops 1610612736 | bytes 9961984 | tf_op jit(solution)/shard_map/while/body/eval_jaxpr/kit,jt->kij/dot_general | solution.py:40
  167.9 1.3 dynamic_slice.107
  170.2 0.2 bitcast_dynamic-update-slice_fusion.18
  171.4 5.4 %fusion.14 = f32[8,8,32,512]{3,2,1,0:T(8,128)} fusion(f32[8,8,32,512]{3,2,1,0:T(8,128)} %get-tuple-element.216, s32[]{:T(128)} %get-tuple-element.215, bf16[8,32,6144]{2,1,0:T(8,128)(2,1)S(1)} %bitcast_dynamic-update-slice_fusion.23, bf16[512,6144]{1,0:T(8,128)(2,1)} %get-tuple-element.245), kind=kOutput, calls=%fused_computation.3.clone.1 | convolution fusion | flops 1610612736 | bytes 9961984 | tf_op jit(solution)/shard_map/while/body/eval_jaxpr/kit,jt->kij/dot_general | solution.py:40
  176.8 5.0 %broadcast_multiply_fusion = f32[8,8,32,512]{3,2,1,0:T(8,128)} fusion(f32[8,8,32,512]{3,2,1,0:T(8,128)} %get-tuple-element.140), kind=kLoop, calls=%fused_computation.12 | loop fusion | flops 1048576 | bytes 8388608 | tf_op jit(solution)/shard_map/mul | solution.py:74
  181.8 7.6 %mul.35 = f32[64,2,16,1,512]{4,3,2,1,0:T(1,128)} reshape(f32[8,8,32,512]{3,2,1,0:T(8,128)} %broadcast_multiply_fusion) | data formatting | bytes 8388608 | tf_op jit(solution)/shard_map/mul | solution.py:74
  (45 shorter events, 7.3 us)
Async XLA Ops:
  6.5 99.0 %all-gather.2.cloned.1.call-start = ((), (), s32[]{:S(2)}) async-start(), calls=%async_computation.1 | async-start | bytes 6488064 | tf_op jit(solution)/shard_map/all_gather | solution.py:66
  19.0 10.0 %all-to-all-start = ((bf16[2,1,16,6144]{3,2,1,0:T(8,128)(2,1)}), bf16[2,1,16,6144]{3,2,1,0:T(8,128)(2,1)S(1)}, u32[]{:S(2)}, u32[]{:S(2)}) async-start(bf16[2,1,16,6144]{3,2,1,0:T(8,128)(2,1)} %broadcast_in_dim.17), calls=%async_computation | async-start | bytes 786432 | tf_op jit(solution)/shard_map/all_to_all | solution.py:15
Sparse Core Ops, SparseCore 0:
  17.5 88.0 all-gather.1
where the time goes:
time: 197 us; the launch traced here: 196 us
  waiting for transfers between devices  83 us (42%)
  matrix products  43.3 us (22%)
  local copies, waits for them, and re-layouts  31.4 us (16%)
  between operations  13.4 us (7%)
  blocking collectives  10.8 us (5%)
  loops' own time  5.92 us (3%)
  other arithmetic  5.04 us (3%)
  starting transfers between devices  3.47 us (2%)
    all_gather x1, waiting for transfers between devices, per_device(): lax.all_gather(whole_time, 'anta', axis=1, tiled=True)  76.5 us
    dot_general x8, matrix products, one_group(): jnp.einsum('kit,jt->kij', stacked, flat_cols, preferred_element_type=jnp....  43.3 us
    all_gather x1, blocking collectives, per_device(): whole_time = lax.all_gather(samples, 'tm', axis=2, tiled=True)  10.8 us
    dynamic_slice x8, local copies, waits for them, and re-layouts, lag_terms(): lax.map(one_group, jnp.arange(lag_count // group_len, dtype=jnp.int32))  10.1 us
    while x56, local copies, waits for them, and re-layouts  9.93 us
    mul x1, local copies, waits for them, and re-layouts, per_device(): return accumulated_sum * factor  7.64 us
    all_to_all x1, waiting for transfers between devices, from_everyone(): return lax.all_to_all(copies, axis, split_axis=0, concat_axis=0, tiled=True)  6.47 us
    another operation x1, loops' own time, lag_terms(): lax.map(one_group, jnp.arange(lag_count // group_len, dtype=jnp.int32))  5.92 us
  transfers between devices with their start and end apart: 2, of which 2 were waited for; matrix products, arithmetic and copies ran while one was open for 1% of the time, Pallas kernels for 0%

commit v1 on v0

v1 whole, which is shorter than its diff:
```python
import functools
import math

import jax
import jax.numpy as jnp
from jax import lax
from jax.experimental import pallas as pl
from jax.experimental.pallas import tpu as pltpu
from jax.sharding import PartitionSpec as P

LAGS = 256
POLS = 2
ROWS = 16
BLOCK = 1536
PHASES = 12
TIMES = 4
NX, NZ, NY = 4, 8, 4
PORTION = 64
TABLE = PORTION + PHASES - 1
WHOLE = (0, 1536)
PART_P = (0, 896)
PART_Q = (896, 1536)
HALF = {
    WHOLE: {1: (0, 768), -1: (768, 1536)},
    PART_P: {1: (0, 512), -1: (512, 896)},
    PART_Q: {1: (896, 1152), -1: (1152, 1536)},
}
DZS = (0, 1, -1, 2, -2, 3, -3, 4)


def kernel_body(x_ref, acc, gathered, rows, table, xt, send_sem, recv_sem):
    tm = lax.axis_index("tm")
    anta = lax.axis_index("anta")
    antb = lax.axis_index("antb")
    y_hi, core = tm // 2, tm % 2
    x, z = anta // NZ, anta % NZ
    y = y_hi * 2 + antb
    tm_partner = y_hi * 2 + (1 - core)
    tm_other = (1 - y_hi) * 2 + core
    tm_last = (1 - y_hi) * 2 + (1 - core)

    def wrap(value, size):
        return lax.rem(value + size, size)

    x_next = {s: wrap(x + s, NX) * NZ + z for s in (1, -1)}
    z_next = {s: x * NZ + wrap(z + s, NZ) for s in (1, -1)}
    z_row = {dz: wrap(z + dz, NZ) * ROWS for dz in range(-4, 5)}

    def at_x(s):
        return {"tm": tm, "anta": x_next[s], "antb": antb}

    def at_z(s):
        return {"tm": tm, "anta": z_next[s], "antb": antb}

    def at_y(s):
        there = wrap(y + s, NY)
        return {"tm": (there // 2) * 2 + core, "anta": anta, "antb": there % 2}

    partner = {"tm": tm_partner, "anta": anta, "antb": antb}
    opposite = {"tm": tm_other, "anta": anta, "antb": antb}

    counter = {}

    def slot(key):
        return counter.setdefault(key, len(counter))

    sent = []

    def copy_of(key, src, dst, device):
        n = slot(key)
        return pltpu.make_async_remote_copy(
            src_ref=src, dst_ref=dst, send_sem=send_sem.at[n], recv_sem=recv_sem.at[n],
            device_id=device, device_id_type=pl.DeviceIdType.MESH,
        )

    def send(key, src, dst, device):
        copy = copy_of(key, src, dst, device)
        copy.start()
        sent.append(copy)

    def wait(key, dst):
        copy_of(key, dst, dst, partner).wait_recv()

    def block(time, rx, dz, lanes):
        row = pl.multiple_of((rx % NX) * (NZ * ROWS) + z_row[dz], ROWS)
        return gathered.at[time, pl.ds(row, ROWS), pl.ds(lanes[0], lanes[1] - lanes[0])]

    def row_block(time, pol):
        return rows.at[time + 1, pl.ds(pl.multiple_of(pol * ROWS, ROWS), ROWS), :]

    def send_z(g, time, s, rx, d):
        lanes = WHOLE if rx == 0 else PART_Q
        if d == 4:
            lanes = HALF[lanes][s]
        ref = block(time, rx, -s * (d - 1), lanes)
        send((g, "z", s, rx, d), ref, ref, at_z(s))

    def send_x(g, time, s, dz, d):
        lanes = WHOLE if dz == 0 else PART_P
        if d == 2:
            lanes = HALF[lanes][s]
        src = block(time, -s * (d - 1), dz, lanes)
        dst = block(time, -s * d, dz, lanes)
        send((g, "x", s, dz, d), src, dst, at_x(s))

    def wait_z(g, time, s, rx, d):
        lanes = WHOLE if rx == 0 else PART_Q
        if d == 4:
            lanes = HALF[lanes][s]
        wait((g, "z", s, rx, d), block(time, rx, -s * d, lanes))

    def wait_x(g, time, s, dz, d):
        lanes = WHOLE if dz == 0 else PART_P
        if d == 2:
            lanes = HALF[lanes][s]
        wait((g, "x", s, dz, d), block(time, -s * d, dz, lanes))

    def start(g, time):
        for s in (1, -1):
            send_z(g, time, s, 0, 1)
        for s in (1, -1):
            send_x(g, time, s, 0, 1)

    def level(g, time, n):
        for rx in (0, 1, 3, 2):
            d = n - {0: 0, 1: 1, 3: 1, 2: 2}[rx]
            if not 1 <= d <= 4:
                continue
            for s in (1, -1):
                wait_z(g, time, s, rx, d)
                if d < 4:
                    send_z(g, time, s, rx, d + 1)
                if rx == 0 and d < 4:
                    for sx in (1, -1):
                        send_x(g, time, sx, -s * d, 1)
            if rx == 0 and d == 4:
                for sx in (1, -1):
                    send_x(g, time, sx, 4, 1)
        for dz in DZS:
            d = n - abs(dz)
            if not 1 <= d <= 2:
                continue
            for s in (1, -1):
                wait_x(g, time, s, dz, d)
                if d == 1:
                    send_x(g, time, s, dz, 2)
                    if dz == 0:
                        for sz in (1, -1):
                            send_z(g, time, sz, -s % NX, 1)
            if dz == 0 and d == 2:
                for sz in (1, -1):
                    send_z(g, time, sz, 2, 1)
        done = {4: (0,), 5: (1, 3), 6: (2,)}.get(n, ())
        for rx in done:
            ref = gathered.at[time, pl.ds(rx * NZ * ROWS, NZ * ROWS), :]
            send((g, "plane", rx), ref, ref, partner)

    def planes(g, time):
        for rx in range(NX):
            wait((g, "plane", rx), gathered.at[time, pl.ds(rx * NZ * ROWS, NZ * ROWS), :])

    barrier = pltpu.get_barrier_semaphore()
    everyone = [at_x(1), at_x(-1), at_z(1), at_z(-1), at_y(1), at_y(-1), opposite, partner]
    for device in everyone:
        pl.semaphore_signal(barrier, inc=1, device_id=device, device_id_type=pl.DeviceIdType.MESH)

    own = x_ref[...].astype(jnp.float32)
    pad = jnp.zeros((128 - ROWS, 128), jnp.float32)
    for tile in range(PHASES):
        piece = jnp.concatenate([own[:, tile * 128:(tile + 1) * 128], pad], 0)
        xt[tile * 128:(tile + 1) * 128, :] = piece.T
    own_row = pl.multiple_of(z * ROWS, ROWS)
    pol_row = pl.multiple_of(antb * ROWS, ROWS)
    for phase in range(PHASES):
        piece = xt[pl.ds(phase, 128, stride=PHASES), :].T[:ROWS, :].astype(jnp.bfloat16)
        lanes = slice(phase * 128, (phase + 1) * 128)
        gathered[tm, pl.ds(own_row, ROWS), lanes] = piece
        rows[tm + 1, pl.ds(pol_row, ROWS), lanes] = piece
    rows[0, :, :] = jnp.zeros((POLS * ROWS, BLOCK), jnp.bfloat16)

    pl.semaphore_wait(barrier, len(everyone))

    own_block = block(tm, 0, 0, WHOLE)
    send("y2", own_block, own_block, opposite)
    start(0, tm)
    for s in (1, -1):
        send(("y", s), own_block, row_block(tm, antb), at_y(s))
    send("own", own_block, row_block(tm, antb), partner)

    level(0, tm, 1)
    wait("y2", block(tm_other, 0, 0, WHOLE))
    start(1, tm_other)
    other_block = block(tm_other, 0, 0, WHOLE)
    send("other", other_block, row_block(tm_other, antb), partner)
    for s in (1, -1):
        there = wrap(y - s, NY)
        ref = row_block((there // 2) * 2 + core, 1 - antb)
        wait(("y", s), ref)
        send(("row", s), ref, ref, partner)
    level(0, tm, 2)
    wait("own", row_block(tm_partner, antb))
    wait("other", row_block(tm_last, antb))
    for s in (1, -1):
        there = wrap(y - s, NY)
        wait(("row", s), row_block((there // 2) * 2 + 1 - core, 1 - antb))
    rows[tm_other + 1, pl.ds(pol_row, ROWS), :] = gathered[tm_other, pl.ds(own_row, ROWS), :]
    level(0, tm, 3)
    level(1, tm_other, 1)

    lane = lax.broadcasted_iota(jnp.int32, (POLS * ROWS, 128), 1)

    def build(n, carry):
        m = PHASES - 1 - n - PORTION * tm + PHASES * 32
        phase, shift = m % PHASES, 32 - m // PHASES
        lanes = pl.ds(pl.multiple_of(phase * 128, 128), 128)
        keep = lane >= shift
        to = pl.ds(pl.multiple_of(n * POLS * ROWS, POLS * ROWS), POLS * ROWS)
        before = pltpu.roll(rows[0, :, lanes], shift, 1)
        for time in range(TIMES):
            now = pltpu.roll(rows[time + 1, :, lanes], shift, 1)
            table[time, to, :] = jnp.where(keep, now, before)
            before = now
        return carry

    lax.fori_loop(0, TABLE, build, 0)

    level(0, tm, 4)
    level(1, tm_other, 2)
    level(0, tm, 5)
    level(1, tm_other, 3)
    level(0, tm, 6)

    half = PORTION * POLS * ROWS // 2
    x_rows = [wrap(a - x + NX, NX) * NZ * ROWS for a in range(NX)]

    def step(u, carry):
        k, part = u // 2, u % 2

        time = jnp.where(k < 2, y_hi, 1 - y_hi) * 2 + jnp.where(k % 2 == 0, core, 1 - core)
        first = part * half
        left = jnp.concatenate([
            table[time, pl.ds(pl.multiple_of(first + (PHASES - 1 - phase) * POLS * ROWS, 32), half), :]
            for phase in range(PHASES)
        ], 1)
        out = pl.ds(pl.multiple_of(first, half), half)
        right = jnp.concatenate([
            gathered[time, pl.ds(pl.multiple_of(row, 128), NZ * ROWS), :] for row in x_rows
        ], 0)
        d = lax.dot_general(left, right, (((1,), (1,)), ((), ())), preferred_element_type=jnp.float32)

        @pl.when(k == 0)
        def _():
            acc[out, :] = d

        @pl.when(k > 0)
        def _():
            acc[out, :] += d
        return carry

    lax.fori_loop(0, 1, step, 0)
    level(1, tm_other, 4)
    lax.fori_loop(1, 2, step, 0)
    planes(0, tm_partner)
    level(1, tm_other, 5)
    lax.fori_loop(2, 3, step, 0)
    level(1, tm_other, 6)
    lax.fori_loop(3, 6, step, 0)
    planes(1, tm_last)
    lax.fori_loop(6, 8, step, 0)
    for copy in sent:
        copy.wait_send()


def per_device(samples):
    m = PORTION * POLS * ROWS
    count = 2 * 68 + 7
    acc = pl.pallas_call(
        kernel_body,
        out_shape=jax.ShapeDtypeStruct((m, 512), jnp.float32),
        in_specs=[pl.BlockSpec(memory_space=pltpu.VMEM)],
        out_specs=pl.BlockSpec(memory_space=pltpu.VMEM),
        scratch_shapes=[
            pltpu.VMEM((TIMES, 512, BLOCK), jnp.bfloat16),
            pltpu.VMEM((TIMES + 1, POLS * ROWS, BLOCK), jnp.bfloat16),
            pltpu.VMEM((TIMES, TABLE * POLS * ROWS, 128), jnp.bfloat16),
            pltpu.VMEM((BLOCK, 128), jnp.float32),
            pltpu.SemaphoreType.DMA((count,)),
            pltpu.SemaphoreType.DMA((count,)),
        ],
        compiler_params=pltpu.CompilerParams(
            collective_id=0, has_side_effects=True, vmem_limit_bytes=40 * 2**20
        ),
        name="gather_correlate",
    )(samples.reshape(ROWS, BLOCK))
    scaled = acc * (1.0 / math.sqrt(BLOCK * TIMES))
    return scaled.reshape(PORTION, POLS, ROWS, 1, 512)


def solution(mesh):
    return jax.shard_map(
        per_device,
        mesh=mesh,
        in_specs=(P("antb", "anta", "tm"),),
        out_specs=P("tm", None, "anta", "antb", None),
        check_vma=False,
    )
```

time: 197 us -> 64.4 us (0.33)
  the two profiles are of different devices: /device:TPU:1 before, /device:TPU:2 now
where the time goes in v1:
time: 64.4 us; the launch traced here: 64.3 us
  Pallas kernels  56.6 us (88%)
  local copies, waits for them, and re-layouts  7.12 us (11%)
    pallas_call x1, Pallas kernels, per_device(): pl.pallas_call(kernel_body, out_shape=jax.ShapeDtypeStruct((m, 512), jnp....  56.6 us
    reshape x1, local copies, waits for them, and re-layouts, per_device(): return scaled.reshape(PORTION, POLS, ROWS, 1, 512)  6.33 us

profile of v1, /device:TPU:2, one launch (start us, length us, event | category | flops | bytes accessed | tf_op | source)
XLA Modules:
  0.0 64.3 jit_solution(11564507414228573887)
XLA Ops:
  0.0 0.0 copy-start
  0.0 0.8 %copy-done = bf16[1,16,1536]{2,1,0:T(8,128)(2,1)S(1)} copy-done((bf16[1,16,1536]{2,1,0:T(8,128)(2,1)S(1)}, bf16[1,16,1536]{2,1,0:T(8,128)(2,1)}, u32[]{:S(2)}) %copy-start) | copy-done | bytes 49176
  0.8 56.6 %gather_correlate.1 = f32[2048,512]{1,0:T(8,128)S(1)} custom-call(bf16[16,1536]{1,0:T(8,128)(2,1)S(1)} %bitcast.2), custom_call_target="tpu_custom_call" | custom-call | tf_op jit(solution)/shard_map/gather_correlate/pallas_call | solution.py:277
  57.4 0.5 broadcast_multiply_fusion
  57.9 6.3 %copy.2 = f32[64,2,16,1,512]{4,3,2,1,0:T(1,128)} copy(f32[64,2,16,1,512]{4,2,1,0,3:T(8,128)S(1)} %bitcast.3) | data formatting | bytes 8388608 | tf_op jit(solution)/shard_map/reshape | solution.py:296
Async XLA Ops:
  0.0 0.8 %copy-start = (bf16[1,16,1536]{2,1,0:T(8,128)(2,1)S(1)}, bf16[1,16,1536]{2,1,0:T(8,128)(2,1)}, u32[]{:S(2)}) copy-start(bf16[1,16,1536]{2,1,0:T(8,128)(2,1)} %param.1) | copy-start | bytes 147460

commit v2 on v0

v2 whole, which is shorter than its diff:
```python
import math

import jax
import jax.numpy as jnp
from jax import lax
from jax.experimental import pallas as pl
from jax.experimental.pallas import tpu as pltpu
from jax.sharding import PartitionSpec as P

POLS = 2
ROWS = 16
BLOCK = 1536
PHASES = 12
TIMES = 4
NX, NZ, NY = 4, 8, 4
PORTION = 64
SCALE = 1.0 / math.sqrt(BLOCK * TIMES)
TABLE = PORTION + PHASES - 1
PAIR = POLS * ROWS
XS = (1, -1, 2)
CHUNKS = ((0, 4, 6), (6, 10, 12), (0, 3, 6))
ROUTES = {2: (0, 0, 0, 0), 3: (0, 0, 2, 2), 4: (0, 1, 2, 2)}
PLAN = (
    "bs", "a1", "b1", "y", "rows", "t0-75", "a2", "cs", "b2", "a3", "wa", "ma01", "c1", "b3", "ma12", "d1",
    "wb", "mb01", "c2", "d2", "mb12", "c3", "d3", "wc", "wd", "mcd02",
)


def halves(lanes):
    low, high = lanes
    middle = (low + high + 1) // 2
    return {1: (low, middle), -1: (middle, high)}


def kernel_body(x_ref, acc, gathered, rows, table, xt, send_sem, recv_sem):
    tm = lax.axis_index("tm")
    anta = lax.axis_index("anta")
    antb = lax.axis_index("antb")
    y_hi, core = tm // 2, tm % 2
    x, z = anta // NZ, anta % NZ
    y = y_hi * 2 + antb
    tm_partner = y_hi * 2 + (1 - core)
    tm_other = (1 - y_hi) * 2 + core
    tm_last = (1 - y_hi) * 2 + (1 - core)

    def wrap(value, size):
        return lax.rem(value + size, size)

    x_next = {s: wrap(x + s, NX) * NZ + z for s in XS}
    z_next = {s: x * NZ + wrap(z + s, NZ) for s in range(-3, 5)}
    z_row = {dz: wrap(z + dz, NZ) * ROWS for dz in range(-4, 5)}

    def at_x(s):
        return {"tm": tm, "anta": x_next[s], "antb": antb}

    def at_z(s):
        return {"tm": tm, "anta": z_next[s], "antb": antb}

    def at_y(s):
        there = wrap(y + s, NY)
        return {"tm": (there // 2) * 2 + core, "anta": anta, "antb": there % 2}

    partner = {"tm": tm_partner, "anta": anta, "antb": antb}
    opposite = {"tm": tm_other, "anta": anta, "antb": antb}

    arrivals, groups, sent = {}, {}, {}

    def copy_of(key, src, dst, device, group):
        n = arrivals.setdefault(key, len(arrivals))
        k = groups.setdefault(group, len(groups))
        return pltpu.make_async_remote_copy(
            src_ref=src, dst_ref=dst, send_sem=send_sem.at[k], recv_sem=recv_sem.at[n],
            device_id=device, device_id_type=pl.DeviceIdType.MESH,
        )

    def send(key, src, dst, device, group):
        copy = copy_of(key, src, dst, device, group)
        copy.start()
        sent[group] = sent.get(group, 0) + math.prod(src.shape) // (ROWS * 128)

    def drain():
        for group, units in sent.items():
            ref = units_of(units)
            copy_of("drain", ref, ref, partner, group).wait_send()

    def units_of(units):
        t, p, r, n = next(
            (t, p, r, n) for t in range(1, TIMES + 1) for p in range(1, NX + 1) for r in range(1, NZ + 1)
            for n in range(1, PHASES + 1) if t * p * r * n == units
        )
        return gathered.at[pl.ds(0, t), pl.ds(0, p), pl.ds(0, r * ROWS), pl.ds(0, n * 128)]

    def size(ref):
        return math.prod(ref.shape) // (ROWS * 128)

    def wait(key, dst):
        copy_of(key, dst, dst, partner, "drain").wait_recv()

    where, kept = {}, []

    def block(time, rx, dz, lanes):
        key = (rx, dz, lanes)
        row = pl.ds(pl.multiple_of(z_row[dz], ROWS), ROWS)
        lanes = pl.ds(lanes[0] * 128, (lanes[1] - lanes[0]) * 128)
        ref = gathered.at[time, rx if isinstance(rx, slice) else rx % NX, row, lanes]
        where[id(ref)] = key
        kept.append(ref)
        return ref

    def row_block(time, pol):
        return rows.at[time + 1, pl.ds(pl.multiple_of(pol * ROWS, ROWS), ROWS), :]

    aside = slice(1, NX)

    def gather_of(g, time, chunk, route, on_landed):
        low, cut, high = chunk
        whole, part_p, part_q = (low, high), (low, cut), (cut, high)
        source = (None,) + ROUTES[route]
        steps = {0: 0}
        for d in (1, 2, 3, 4):
            steps[d] = steps[source[d]] + 1

        def z_lanes(s, rx, d):
            lanes = whole if rx == 0 else part_q
            if d < 4:
                return lanes
            if source[4] == 0:
                return lanes if s == 1 else (high, high)
            return halves(lanes)[s]

        def send_z(s, rx, d):
            lanes = z_lanes(s, rx, d)
            if lanes[0] < lanes[1]:
                ref = block(time, rx, -s * source[d], lanes)
                send((g, steps[d] + (rx is aside), "z", s), ref, ref, at_z(s * (d - source[d])), (g, "z", rx is aside))

        def send_x(dz):
            lanes = whole if dz == 0 else part_p
            for s in XS:
                send((g, steps[abs(dz)] + 1, "x", s), block(time, 0, dz, lanes), block(time, -s, dz, lanes), at_x(s), (g, "x", dz == 0))

        def send_on(rx, s, at):
            for d in (1, 2, 3, 4):
                if source[d] == at:
                    send_z(s, rx, d)

        def wait_link(n, link, s, refs):
            wait((g, n, link, s), units_of(sum(size(ref) for ref in refs)))

        def z_refs(n, s):
            refs = []
            for rx, late in ((0, 0), (aside, 1)):
                for d in (1, 2, 3, 4):
                    lanes = z_lanes(s, rx, d)
                    if steps[d] + late == n and lanes[0] < lanes[1]:
                        refs.append(block(time, rx, -s * d, lanes))
            return refs

        def x_refs(n, s):
            return [
                block(time, -s, dz, part_p if dz else whole)
                for dz in (0, 1, -1, 2, -2, 3, -3, 4) if steps[abs(dz)] + 1 == n
            ]

        def start():
            for s in (1, -1):
                send_on(0, s, 0)
            send_x(0)
            on_landed(block(time, 0, 0, whole))

        def level(n):
            landed = []
            for s in (1, -1):
                refs = z_refs(n, s)
                if refs:
                    wait_link(n, "z", s, refs)
                    landed.extend(refs)
                for d in (1, 2, 3, 4):
                    if steps[d] == n:
                        send_on(0, s, d)
                    if steps[d] == n - 1:
                        send_on(aside, s, d)
                    if steps[d] == n and d < 4:
                        send_x(-s * d)
            if steps[4] == n:
                send_x(4)
            for s in XS:
                refs = x_refs(n, s)
                if refs:
                    wait_link(n, "x", s, refs)
                    landed.extend(refs)
            if n == 1:
                for s in (1, -1):
                    send_on(aside, s, 0)
            for ref in landed:
                on_landed(ref)
            if g == "b":
                marks.append(len(crossed))

        return start, level

    def to_core(g):
        def on_landed(ref):
            send((g, "core"), ref, ref, partner, (g, "core"))
        return on_landed

    crossed, marks = [], [0]

    def to_core_and_across(ref):
        send(("b", "core"), ref, ref, partner, ("b", "core"))
        if where[id(ref)][:2] != (0, 0):
            send(("d", len(marks)), ref, ref, opposite, ("d", "y", len(marks)))
            crossed.append(where[id(ref)])

    def landed_core(g):
        time, (low, _, high) = cores[g]
        wait((g, "core"), gathered.at[time, :, :, pl.ds(low * 128, (high - low) * 128)])

    gathers = {
        "a": gather_of("a", tm, CHUNKS[0], 3, to_core("a")),
        "b": gather_of("b", tm, CHUNKS[1], 3, to_core_and_across),
        "c": gather_of("c", tm_other, CHUNKS[2], 3, to_core("c")),
    }
    cores = {
        "a": (tm_partner, CHUNKS[0]), "b": (tm_partner, CHUNKS[1]),
        "c": (tm_last, CHUNKS[0]), "d": (tm_last, CHUNKS[1]),
    }

    def take_across(n):
        refs = [block(tm_other, *key) for key in crossed[marks[n - 1]:marks[n]]]
        wait(("d", n), units_of(sum(size(ref) for ref in refs)))
        for ref in refs:
            send(("d", "core"), ref, ref, partner, ("d", "core"))

    lane = lax.broadcasted_iota(jnp.int32, (PAIR, 128), 1)

    def build(n, carry):
        m = PHASES - 1 - n - PORTION * tm + PHASES * 32
        phase, shift = m % PHASES, 32 - m // PHASES
        lanes = pl.ds(pl.multiple_of(phase * 128, 128), 128)
        keep = lane >= shift
        to = pl.ds(pl.multiple_of(n * PAIR, PAIR), PAIR)
        before = pltpu.roll(rows[0, :, lanes], shift, 1)
        for time in range(TIMES):
            now = pltpu.roll(rows[time + 1, :, lanes], shift, 1)
            table[time, to, :] = jnp.where(keep, now, before)
            before = now
        return carry

    def build_part(low, high):
        lax.fori_loop(low, high, build, 0, unroll=5)

    half = PORTION * PAIR // 2
    planes = [wrap(a - x + NX, NX) for a in range(NX)]

    first_product, last_product = 'a', 'cd'

    def product(g):
        taken = [
            (time, cores[k][1][0], cores[k][1][2]) for k in g
            for time in ((tm, tm_partner) if k in "ab" else (tm_other, tm_last))
        ]

        def step(part, carry):
            first = part * half
            left = jnp.concatenate([
                table[time, pl.ds(pl.multiple_of(first + (PHASES - 1 - phase) * PAIR, PAIR), half), :]
                for time, low, high in taken for phase in range(low, high)
            ], 1)
            right = jnp.concatenate([
                jnp.concatenate([gathered[time, plane, :, pl.ds(low * 128, (high - low) * 128)] for time, low, high in taken], 1)
                for plane in planes
            ], 0)
            d = lax.dot_general(left, right, (((1,), (1,)), ((), ())), preferred_element_type=jnp.float32)
            for tile in range(4):
                to = pl.ds(4 * first + tile, half, stride=4)
                piece = d[:, tile * 128:(tile + 1) * 128]
                if g == first_product:
                    acc[to, :] = piece
                elif g != last_product:
                    acc[to, :] += piece
                else:
                    acc[to, :] = (acc[to, :] + piece) * SCALE
            return carry

        return step

    barrier = pltpu.get_barrier_semaphore()
    everyone = [at_x(s) for s in XS] + [at_z(s) for s in range(-3, 5) if s] + [at_y(1), at_y(-1), opposite, partner]
    for device in everyone:
        pl.semaphore_signal(barrier, inc=1, device_id=device, device_id_type=pl.DeviceIdType.MESH)
    own = x_ref[...].astype(jnp.float32)
    pad = jnp.zeros((128 - ROWS, 128), jnp.float32)
    for tile in range(PHASES):
        piece = jnp.concatenate([own[:, tile * 128:(tile + 1) * 128], pad], 0)
        xt[tile * 128:(tile + 1) * 128, :] = piece.T
    own_row = pl.multiple_of(z * ROWS, ROWS)
    pol_row = pl.multiple_of(antb * ROWS, ROWS)
    for phase in range(PHASES):
        piece = xt[pl.ds(phase, 128, stride=PHASES), :].T[:ROWS, :].astype(jnp.bfloat16)
        lanes = slice(phase * 128, (phase + 1) * 128)
        gathered[tm, 0, pl.ds(own_row, ROWS), lanes] = piece
        rows[tm + 1, pl.ds(pol_row, ROWS), lanes] = piece
    rows[0, :, :] = jnp.zeros((PAIR, BLOCK), jnp.bfloat16)
    pl.semaphore_wait(barrier, len(everyone))

    full = (0, PHASES)
    own_block = block(tm, 0, 0, full)

    def step_y():
        other_block = block(tm_other, 0, 0, full)
        wait("y2", other_block)
        send("other", other_block, row_block(tm_other, antb), partner, "rows")
        rows[tm_other + 1, pl.ds(pol_row, ROWS), :] = gathered[tm_other, 0, pl.ds(own_row, ROWS), :]
        for s in (1, -1):
            there = wrap(y - s, NY)
            ref = row_block((there // 2) * 2 + core, 1 - antb)
            wait(("y", s), ref)
            send(("row", s), ref, ref, partner, "rows")

    def start_c():
        gathers["c"][0]()
        d_own = block(tm_other, 0, 0, (CHUNKS[1][0], CHUNKS[1][2]))
        send(("d", "core"), d_own, d_own, partner, ("d", "core"))

    def step_rows():
        wait("own", row_block(tm_partner, antb))
        wait("other", row_block(tm_last, antb))
        for s in (1, -1):
            there = wrap(y - s, NY)
            wait(("row", s), row_block((there // 2) * 2 + 1 - core, 1 - antb))

    send("y2", own_block, own_block, opposite, "rows")
    for s in (1, -1):
        send(("y", s), own_block, row_block(tm, antb), at_y(s), "rows")
    gathers["a"][0]()
    send("own", own_block, row_block(tm, antb), partner, "rows")

    for word in PLAN:
        if word == "y":
            step_y()
        elif word == "cs":
            start_c()
        elif word == "bs":
            gathers["b"][0]()
        elif word == "rows":
            step_rows()
        elif word[0] == "t":
            low, high = word[1:].split("-")
            build_part(int(low), int(high))
        elif word[0] == "d":
            take_across(int(word[1]))
        elif word[0] == "w":
            landed_core(word[1])
        elif word[0] == "m":
            lax.fori_loop(int(word[-2]), int(word[-1]), product(word[1:-2]), 0)
        else:
            gathers[word[0]][1](int(word[1]))
    drain()


def per_device(samples):
    m = PORTION * PAIR
    acc = pl.pallas_call(
        kernel_body,
        out_shape=jax.ShapeDtypeStruct((m * 4, 128), jnp.float32),
        in_specs=[pl.BlockSpec(memory_space=pltpu.VMEM)],
        out_specs=pl.BlockSpec(memory_space=pltpu.VMEM),
        scratch_shapes=[
            pltpu.VMEM((TIMES, NX, NZ * ROWS, BLOCK), jnp.bfloat16),
            pltpu.VMEM((TIMES + 1, PAIR, BLOCK), jnp.bfloat16),
            pltpu.VMEM((TIMES, TABLE * PAIR, 128), jnp.bfloat16),
            pltpu.VMEM((BLOCK, 128), jnp.float32),
            pltpu.SemaphoreType.DMA((24,)),
            pltpu.SemaphoreType.DMA((64,)),
        ],
        compiler_params=pltpu.CompilerParams(
            collective_id=0, has_side_effects=True, vmem_limit_bytes=40 * 2**20
        ),
        name="gather_correlate",
    )(samples.reshape(ROWS, BLOCK))
    return acc.reshape(PORTION, POLS, ROWS, 1, 512)


def solution(mesh):
    return jax.shard_map(
        per_device,
        mesh=mesh,
        in_specs=(P("antb", "anta", "tm"),),
        out_specs=P("tm", None, "anta", "antb", None),
        check_vma=False,
    )
```

time: 197 us -> 48.6 us (0.25)
  waiting for transfers between devices: 83 us -> 0 us
  Pallas kernels: 0 us -> 45.7 us
  matrix products: 43.3 us -> 0 us
  local copies, waits for them, and re-layouts: 31.4 us -> 2.81 us
  between operations: 13.4 us -> 0.01 us
  blocking collectives: 10.8 us -> 0 us
  loops' own time: 5.92 us -> 0 us
  other arithmetic: 5.04 us -> 0 us
  starting transfers between devices: 3.47 us -> 0 us
    all_gather x1 -> x0, waiting for transfers between devices: 76.5 us -> none  [per_device(): lax.all_gather(whole_time, 'anta', axis=1, tiled=True)]
    pallas_call x0 -> x1, Pallas kernels: none -> 45.7 us  [per_device(): pl.pallas_call(kernel_body, out_shape=jax.ShapeDtypeStruct((m * 4, 128),...]
    dot_general x8 -> x0, matrix products: 43.3 us -> none  [one_group(): jnp.einsum('kit,jt->kij', stacked, flat_cols, preferred_element_type=jnp....]
    all_gather x1 -> x0, blocking collectives: 10.8 us -> none  [per_device(): whole_time = lax.all_gather(samples, 'tm', axis=2, tiled=True)]
    dynamic_slice x8 -> x0, local copies, waits for them, and re-layouts: 10.1 us -> none  [lag_terms(): lax.map(one_group, jnp.arange(lag_count // group_len, dtype=jnp.int32))]
    while x56 -> x0, local copies, waits for them, and re-layouts: 9.93 us -> none
    mul x1 -> x0, local copies, waits for them, and re-layouts: 7.64 us -> none  [per_device(): return accumulated_sum * factor]
    all_to_all x1 -> x0, waiting for transfers between devices: 6.47 us -> none  [from_everyone(): return lax.all_to_all(copies, axis, split_axis=0, concat_axis=0, tiled=True)]
  transfers between devices with their start and end apart: 2 -> 0, of which waited for: 2 -> 0; matrix products, arithmetic and copies ran while one was open for 1% -> 0% of each run, Pallas kernels for 0% -> 0%
where the time goes in v2:
time: 48.6 us; the launch traced here: 48.5 us
  Pallas kernels  45.7 us (94%)
  local copies, waits for them, and re-layouts  2.81 us (6%)
    pallas_call x1, Pallas kernels, per_device(): pl.pallas_call(kernel_body, out_shape=jax.ShapeDtypeStruct((m * 4, 128),...  45.7 us
    unnamed x3, local copies, waits for them, and re-layouts  2.81 us

profile of v2, /device:TPU:1, one launch (start us, length us, event | category | flops | bytes accessed | tf_op | source)
XLA Modules:
  0.0 48.5 jit_solution(15954401837472944737)
XLA Ops:
  0.0 0.0 copy-start
  0.0 0.8 %copy-done = bf16[1,16,1536]{2,1,0:T(8,128)(2,1)S(1)} copy-done((bf16[1,16,1536]{2,1,0:T(8,128)(2,1)S(1)}, bf16[1,16,1536]{2,1,0:T(8,128)(2,1)}, u32[]{:S(2)}) %copy-start) | copy-done | bytes 49176
  0.8 45.7 %gather_correlate.1 = f32[8192,128]{1,0:T(8,128)S(1)} custom-call(bf16[16,1536]{1,0:T(8,128)(2,1)S(1)} %bitcast.3), custom_call_target="tpu_custom_call" | custom-call | tf_op jit(solution)/shard_map/gather_correlate/pallas_call | solution.py:364
  46.5 2.0 %copy.4 = f32[64,2,16,1,512]{4,3,2,1,0:T(1,128)} copy(f32[64,2,16,1,512]{4,3,2,1,0:T(1,128)S(1)} %bitcast.2) | data formatting | bytes 8388608
Async XLA Ops:
  0.0 0.8 %copy-start = (bf16[1,16,1536]{2,1,0:T(8,128)(2,1)S(1)}, bf16[1,16,1536]{2,1,0:T(8,128)(2,1)}, u32[]{:S(2)}) copy-start(bf16[1,16,1536]{2,1,0:T(8,128)(2,1)} %param.1) | copy-start | bytes 147460
